TPU v7x, 128 devices: a whole 4x4x4 slice. The times are simulated.
128 devices in a mesh: col: 2 (over core), row: 64 (over z, y, x).
Axes of the slice: x: 4, y: 4, z: 4, core: 2. Of those that a mesh axis runs over, the one named last changes fastest.
Arguments:
- w_gate: float32 [512, 1024], P('row', 'col')
- w_up: float32 [512, 1024], P('row', 'col')
- w_down: float32 [1024, 512], P('row', 'col')
- x_norm: bfloat16 [32768, 512], P(None, 'row')
- x_act: bfloat16 [32768, 1024], P(None, 'row')
- dy_gate: bfloat16 [32768, 1024], P(None, 'col')
- dy_up: bfloat16 [32768, 1024], P(None, 'col')
- dy_down: bfloat16 [32768, 512], P(None, 'col')
- r_gate: float32 [512], P('row')
- c_gate: float32 [1024], P('col')
- r_up: float32 [512], P('row')
- c_up: float32 [1024], P('col')
- r_down: float32 [1024], P('row')
- c_down: float32 [512], P('col')
- hyper_params: float32 [3], replicated
Outputs:
- output 1: float32 [512, 1024], P('row', 'col')
- output 2: float32 [512, 1024], P('row', 'col')
- output 3: float32 [1024, 512], P('row', 'col')
- output 4: float32 [512], P('row')
- output 5: float32 [1024], P('col')
- output 6: float32 [512], P('row')
- output 7: float32 [1024], P('col')
- output 8: float32 [1024], P('row')
- output 9: float32 [512], P('col')
- output 10: bfloat16 [32768, 512], P(None, 'row')
- output 11: bfloat16 [32768, 1024], P(None, 'row')
All inputs are finite; a program needn't handle non-finite values.
Results may differ from a plain program's by a relative error of at most 0.001.
Values are sent between devices in bfloat16 or wider.
A program may use at most 1 GiB of HBM per device.

v0:
```python
import jax
import jax.numpy as jnp
from jax import lax
from jax.sharding import PartitionSpec as P

EPS_ONE = 1e-30
EPS_TWO = 1e-3


def factored_step(w_loc, grad_loc, r_loc, c_loc, hyper_params, m_total, n_total):
    beta_two = hyper_params[0]
    grad_sq = grad_loc * grad_loc + EPS_ONE
    row_sum = lax.psum(jnp.sum(grad_sq, axis=1), 'col')
    col_sum = lax.psum(jnp.sum(grad_sq, axis=0), 'row')
    r_new = beta_two * r_loc + (1.0 - beta_two) * (row_sum / n_total)
    c_new = beta_two * c_loc + (1.0 - beta_two) * (col_sum / m_total)
    r_mean = lax.psum(jnp.sum(r_new), 'row') / m_total
    update = grad_loc * lax.rsqrt(r_new[:, None] * c_new[None, :] / r_mean)
    u_sq = lax.psum(jnp.sum(update * update), ('row', 'col'))
    rms_u = jnp.sqrt(u_sq / (m_total * n_total))
    update_hat = update / jnp.maximum(1.0, rms_u / hyper_params[2])
    w_sq = lax.psum(jnp.sum(w_loc * w_loc), ('row', 'col'))
    step_size = hyper_params[1] * jnp.maximum(EPS_TWO, jnp.sqrt(w_sq / (m_total * n_total)))
    return w_loc - step_size * update_hat, r_new, c_new


def weight_grad(activations, grad_out):
    return lax.dot_general(activations, grad_out, (((0,), (0,)), ((), ())), preferred_element_type=jnp.float32)


def input_grad(grad_out, weight):
    return lax.dot_general(grad_out, weight.astype(jnp.bfloat16), (((1,), (1,)), ((), ())), preferred_element_type=jnp.float32)


def solution(mesh):
    row_size = mesh.shape['row']
    col_size = mesh.shape['col']
    weight_spec = P('row', 'col')
    act_spec = P(None, 'row')
    grad_spec = P(None, 'col')
    in_specs = (weight_spec,) * 3 + (act_spec, act_spec) + (grad_spec,) * 3 + (P('row'), P('col')) * 3 + (P(),)
    out_specs = (weight_spec,) * 3 + (P('row'), P('col')) * 3 + (act_spec, act_spec)

    def body(w_gate, w_up, w_down, x_norm, x_act, dy_gate, dy_up, dy_down, r_gate, c_gate, r_up, c_up, r_down, c_down, hyper_params):
        d_model = w_gate.shape[0] * row_size
        d_ff = w_gate.shape[1] * col_size
        new_gate, r_gate_new, c_gate_new = factored_step(w_gate, weight_grad(x_norm, dy_gate), r_gate, c_gate, hyper_params, d_model, d_ff)
        new_up, r_up_new, c_up_new = factored_step(w_up, weight_grad(x_norm, dy_up), r_up, c_up, hyper_params, d_model, d_ff)
        new_down, r_down_new, c_down_new = factored_step(w_down, weight_grad(x_act, dy_down), r_down, c_down, hyper_params, d_ff, d_model)
        dx_norm = lax.psum(input_grad(dy_gate, w_gate) + input_grad(dy_up, w_up), 'col').astype(jnp.bfloat16)
        dx_act = lax.psum(input_grad(dy_down, w_down), 'col').astype(jnp.bfloat16)
        return (new_gate, new_up, new_down, r_gate_new, c_gate_new, r_up_new, c_up_new, r_down_new, c_down_new, dx_norm, dx_act)

    return jax.shard_map(body, mesh=mesh, in_specs=in_specs, out_specs=out_specs, check_vma=False)
```

profile of v0, /device:TPU:1, one launch (start us, length us, event | category | flops | bytes accessed | tf_op | source)
XLA Modules:
  0.0 358.6 jit_solution(13972195272195825498)
XLA Ops:
  0.7 15.1 %fusion.2 = (f32[512]{0:T(512)S(1)}, f32[8]{0:T(128)S(1)}, f32[8,512]{1,0:T(8,128)S(1)}) fusion(bf16[32768,8]{0,1:T(8,128)(2,1)} %param.18, bf16[32768,512]{1,0:T(8,128)(2,1)} %param.21), kind=kOutput, calls=%fused_computation.18 | convolution fusion | flops 268451328 | bytes 34097184 | tf_op jit(solution)/shard_map/dot_general | solution.py:28
  15.8 13.0 %fusion = (f32[512]{0:T(512)S(1)}, f32[8]{0:T(128)S(1)}, f32[8,512]{1,0:T(8,128)S(1)}) fusion(bf16[32768,8]{0,1:T(8,128)(2,1)S(1)} %copy-done.2, bf16[32768,512]{1,0:T(8,128)(2,1)} %param.20), kind=kOutput, calls=%fused_computation.16 | convolution fusion | flops 268451328 | bytes 34097184 | tf_op jit(solution)/shard_map/dot_general | solution.py:28
  28.8 8.2 %fusion.4 = (f32[256]{0:T(256)S(1)}, f32[16]{0:T(128)S(1)}, f32[16,256]{1,0:T(8,128)S(1)}) fusion(bf16[32768,16]{0,1:T(8,128)(2,1)S(1)} %copy-done, bf16[32768,256]{1,0:T(8,128)(2,1)} %param.22), kind=kOutput, calls=%fused_computation.20 | convolution fusion | flops 268451584 | bytes 17843264 | tf_op jit(solution)/shard_map/dot_general | solution.py:28
  37.0 10.2 %fusion.6 = f32[32768,16]{0,1:T(8,128)S(1)} fusion(bf16[32768,256]{1,0:T(8,128)(2,1)} %param.22, f32[16,256]{1,0:T(8,128)S(1)} %copy-done.5), kind=kOutput, calls=%fused_computation.22 | convolution fusion | flops 268439552 | bytes 18890752 | tf_op jit(solution)/shard_map/dot_general | solution.py:32
  47.2 15.1 %fusion.9 = f32[32768,8]{0,1:T(8,128)S(1)} fusion(bf16[32768,512]{1,0:T(8,128)(2,1)} %param.20, f32[8,512]{1,0:T(8,128)S(1)} %copy-done.4), kind=kOutput, calls=%fused_computation.25 | convolution fusion | flops 268439552 | bytes 34619392 | tf_op jit(solution)/shard_map/dot_general | solution.py:32
  62.3 0.0 copy-start.16
  62.4 16.1 %convolution_add_fusion = f32[32768,8]{0,1:T(8,128)} fusion(f32[32768,8]{0,1:T(8,128)S(1)} %fusion.9, bf16[32768,512]{1,0:T(8,128)(2,1)} %param.21, f32[8,512]{1,0:T(8,128)S(1)} %copy-done.3), kind=kOutput, calls=%fused_computation | convolution fusion | flops 268701696 | bytes 35667968 | tf_op jit(solution)/shard_map/dot_general | solution.py:32
  78.4 13.7 %all-reduce.4 = (f32[8]{0:T(128)S(1)}, f32[8]{0:T(128)S(1)}, f32[16]{0:T(128)S(1)}, bf16[32768,8]{0,1:T(8,128)(2,1)}, bf16[32768,16]{0,1:T(8,128)(2,1)}) all-reduce(f32[8]{0:T(128)S(1)} %get-tuple-element.16, f32[8]{0:T(128)S(1)} %get-tuple-element.14, f32[16]{0:T(128)S(1)} %get-tuple-element.12, ...), channel_id=1, replica_groups=mesh['col'=2,'row'=64] {'col'}, use_global_device_ids=true, to_apply=%region_3.0 | all-reduce | flops 786464 | bytes 4718848 | tf_op jit(solution)/shard_map/psum | solution.py:13
  92.2 0.7 fusion.14
  93.5 1.2 fusion.12
  94.8 1.2 fusion.11
  96.0 155.6 %all-reduce.1 = (f32[]{:T(128)}, f32[512]{0:T(512)S(1)}, f32[]{:T(128)}, f32[512]{0:T(512)S(1)}, f32[]{:T(128)}, /*index=5*/f32[256]{0:T(256)S(1)}) all-reduce(f32[]{:T(128)} %get-tuple-element.46, f32[512]{0:T(512)S(1)} %get-tuple-element.15, f32[]{:T(128)} %get-tuple-element.36, ...), channel_id=1, replica_groups=mesh['col'=2,'row'=64] {'row'}, use_global_device_ids=true, to_apply=%region_7.0 | all-reduce | flops 1283 | bytes 10264 | tf_op jit(solution)/shard_map/psum | solution.py:17
  251.7 0.6 multiply_add_fusion.5
  253.0 0.7 multiply_reduce_fusion
  253.7 0.6 multiply_add_fusion.3
  254.9 0.7 multiply_reduce_fusion.2
  255.6 0.6 multiply_add_fusion.4
  256.9 0.7 multiply_reduce_fusion.4
  257.6 0.6 multiply_reduce_fusion.3
  258.2 0.6 multiply_reduce_fusion.1
  258.8 89.6 %all-reduce = (f32[]{:T(128)}, f32[]{:T(128)}, f32[]{:T(128)}, f32[]{:T(128)}, f32[]{:T(128)}, /*index=5*/f32[]{:T(128)}) all-reduce(f32[]{:T(128)} %multiply_reduce_fusion.4, f32[]{:T(128)} %get-tuple-element.49, f32[]{:T(128)} %multiply_reduce_fusion.2, f32[]{:T(128)} %get-tuple-element.48, ...), channel_id=1, replica_groups=mesh['col'=2,'row'=64] {'row','col'}, use_global_device_ids=true, to_apply=%region_9.0 | all-reduce | flops 6 | bytes 48 | tf_op jit(solution)/shard_map/psum | solution.py:19
  351.0 0.7 multiply_subtract_fusion
  354.4 0.7 multiply_subtract_fusion.1
  357.8 0.7 multiply_subtract_fusion.2
  (37 shorter events, 0.1 us)
Async XLA Ops:
  0.6 28.1 %copy-start = (bf16[32768,16]{0,1:T(8,128)(2,1)S(1)}, bf16[32768,16]{0,1:T(8,128)(2,1)}, u32[]{:S(2)}) copy-start(bf16[32768,16]{0,1:T(8,128)(2,1)} %param.19) | copy-start | bytes 3145732
  0.7 15.1 %copy-start.2 = (bf16[32768,8]{0,1:T(8,128)(2,1)S(1)}, bf16[32768,8]{0,1:T(8,128)(2,1)}, u32[]{:S(2)}) copy-start(bf16[32768,8]{0,1:T(8,128)(2,1)} %param.18) | copy-start | bytes 1572868
  15.8 21.2 %copy-start.5 = (f32[16,256]{1,0:T(8,128)S(1)}, f32[16,256]{1,0:T(8,128)}, u32[]{:S(2)}) copy-start(f32[16,256]{1,0:T(8,128)} %param.17) | copy-start | bytes 49156
  28.8 18.4 %copy-start.4 = (f32[8,512]{1,0:T(8,128)S(1)}, f32[8,512]{1,0:T(8,128)}, u32[]{:S(2)}) copy-start(f32[8,512]{1,0:T(8,128)} %param.15) | copy-start | bytes 49156
  37.0 25.3 %copy-start.3 = (f32[8,512]{1,0:T(8,128)S(1)}, f32[8,512]{1,0:T(8,128)}, u32[]{:S(2)}) copy-start(f32[8,512]{1,0:T(8,128)} %param.16) | copy-start | bytes 49156
  47.2 311.4 %copy-start.1 = (bf16[32768,16]{0,1:T(8,128)(2,1)S(1)}, bf16[32768,16]{0,1:T(8,128)(2,1)}, u32[]{:S(2)}) copy-start(bf16[32768,16]{0,1:T(8,128)(2,1)} %param.19) | copy-start | bytes 3145732
  62.3 29.9 %copy-start.10 = (f32[3]{0:T(128)S(1)}, f32[3]{0:T(128)}, u32[]{:S(2)}) copy-start(f32[3]{0:T(128)} %param.29) | copy-start | bytes 40
  62.3 31.2 %copy-start.16 = (f32[8]{0:T(128)S(1)}, f32[8]{0:T(128)}, u32[]{:S(2)}) copy-start(f32[8]{0:T(128)} %param.25) | copy-start | bytes 100
  62.3 31.2 %copy-start.17 = (f32[8]{0:T(128)S(1)}, f32[8]{0:T(128)}, u32[]{:S(2)}) copy-start(f32[8]{0:T(128)} %param.23) | copy-start | bytes 100
  62.3 32.4 %copy-start.18 = (f32[16]{0:T(128)S(1)}, f32[16]{0:T(128)}, u32[]{:S(2)}) copy-start(f32[16]{0:T(128)} %param.27) | copy-start | bytes 196
  62.3 189.3 %copy-start.15 = (f32[256]{0:T(256)S(1)}, f32[256]{0:T(256)}, u32[]{:S(2)}) copy-start(f32[256]{0:T(256)} %param.28) | copy-start | bytes 3076
  62.3 191.3 %copy-start.13 = (f32[512]{0:T(512)S(1)}, f32[512]{0:T(512)}, u32[]{:S(2)}) copy-start(f32[512]{0:T(512)} %param.26) | copy-start | bytes 6148
  62.3 193.3 %copy-start.14 = (f32[512]{0:T(512)S(1)}, f32[512]{0:T(512)}, u32[]{:S(2)}) copy-start(f32[512]{0:T(512)} %param.24) | copy-start | bytes 6148
  94.8 263.8 %copy-start.11 = (f32[8]{0:T(128)}, f32[8]{0:T(128)S(1)}, u32[]{:S(2)}) copy-start(f32[8]{0:T(128)S(1)} %get-tuple-element.37) | copy-start | bytes 100
  94.8 263.8 %copy-start.12 = (f32[8]{0:T(128)}, f32[8]{0:T(128)S(1)}, u32[]{:S(2)}) copy-start(f32[8]{0:T(128)S(1)} %get-tuple-element.47) | copy-start | bytes 100
  96.0 262.5 %copy-start.9 = (f32[16]{0:T(128)}, f32[16]{0:T(128)S(1)}, u32[]{:S(2)}) copy-start(f32[16]{0:T(128)S(1)} %get-tuple-element.35) | copy-start | bytes 196
  252.3 106.2 %copy-start.8 = (f32[256]{0:T(256)}, f32[256]{0:T(256)S(1)}, u32[]{:S(2)}) copy-start(f32[256]{0:T(256)S(1)} %multiply_add_fusion.5) | copy-start | bytes 3076
  254.3 104.2 %copy-start.6 = (f32[512]{0:T(512)}, f32[512]{0:T(512)S(1)}, u32[]{:S(2)}) copy-start(f32[512]{0:T(512)S(1)} %multiply_add_fusion.3) | copy-start | bytes 6148
  256.3 102.3 %copy-start.7 = (f32[512]{0:T(512)}, f32[512]{0:T(512)S(1)}, u32[]{:S(2)}) copy-start(f32[512]{0:T(512)S(1)} %multiply_add_fusion.4) | copy-start | bytes 6148
where the time goes:
time: 359 us
  blocking collectives  259 us (72%)
  matrix products  77.6 us (22%)
  between operations  11.4 us (3%)
  other arithmetic  9.8 us (3%)
    psum x1, blocking collectives, factored_step(): r_mean = lax.psum(jnp.sum(r_new), 'row') / m_total  156 us
    psum x1, blocking collectives, factored_step(): u_sq = lax.psum(jnp.sum(update * update), ('row', 'col'))  89.6 us
    dot_general x3, matrix products, input_grad(): lax.dot_general(grad_out, weight.astype(jnp.bfloat16), (((1,), (1,)), (()...  41.4 us
    dot_general x3, matrix products, weight_grad(): lax.dot_general(activations, grad_out, (((0,), (0,)), ((), ())), preferre...  36.3 us
    psum x1, blocking collectives, factored_step(): row_sum = lax.psum(jnp.sum(grad_sq, axis=1), 'col')  13.7 us

commit v1 on v0

v1 whole, which is shorter than its diff:
```python
import functools

import jax
import jax.numpy as jnp
from jax import lax
from jax.experimental import pallas as pl
from jax.experimental.pallas import tpu as pltpu
from jax.sharding import PartitionSpec as P

EPS_ONE = 1e-30
EPS_TWO = 1e-3
MESH = pl.DeviceIdType.MESH
BF16 = jnp.bfloat16
F32 = jnp.float32


def dot_nt(lhs, rhs):
    return lax.dot_general(lhs, rhs, (((1,), (1,)), ((), ())), preferred_element_type=F32)


def dot_nn(lhs, rhs):
    return lax.dot_general(lhs, rhs, (((1,), (0,)), ((), ())), preferred_element_type=F32)


def to_column(row_ref):
    m = row_ref.shape[1]
    eye = lax.broadcasted_iota(jnp.int32, (m, m), 0) == lax.broadcasted_iota(jnp.int32, (m, m), 1)
    spread = jnp.where(eye, jnp.broadcast_to(row_ref[...], (m, m)), 0.0)
    return jnp.broadcast_to(jnp.sum(spread, axis=1, keepdims=True), (m, 128))


def to_row(column):
    m = column.shape[0]
    eye = lax.broadcasted_iota(jnp.int32, (m, m), 0) == lax.broadcasted_iota(jnp.int32, (m, m), 1)
    return jnp.sum(jnp.where(eye, column[:, :m], 0.0), axis=0, keepdims=True)


def widen(column, n):
    return jnp.concatenate([column] * (n // 128), axis=1)


def step_kernel(
    dims,
    hyper, w_gate, w_up, w_down, xn, xa, dyg, dyu, dyd, r_gate, c_gate, r_up, c_up, r_down, c_down,
    w_gate_o, w_up_o, w_down_o, r_gate_o, c_gate_o, r_up_o, c_up_o, r_down_o, c_down_o, dxn_o, dxa_o,
    dyg_v, dyu_v, dya_v, dyb_v,
    wn_v, wa_v, wb_v, wlg_v, wlu_v,
    xrn, xra, xrb, xln,
    dsn, dsa, dsb, dkn, dka, dkb, drn, dra, drb, fin_n, fin_a, fin_b,
    gpn, gpa, gpb, grn, gra, grb,
    rs_v, rr_v, st_v, sr_v, fs_v, fr_v,
    ldg, ldu, lda, ldb, ldx,
    w_ss, w_rs, x_ss, x_rs, xf_ss, xf_rs, p_ss, p_rs, d_ss, d_rs, o_ss, o_rs, o_ls, f_ss, f_rs,
    g_ss, g_rs, r_ss, r_rs, s_ss, s_rs, e_ss, e_rs,
):
    ring, cores, tokens = dims
    m, nf = w_gate.shape
    ma, nd = w_down.shape
    tq = tokens // ring
    th = tq // 2
    aq = tq // 2
    ah = aq // 2
    ct = min(2048, th)
    n_ct = th // ct
    rows = ring**3

    core = lax.axis_index("col")
    row = lax.axis_index("row")
    partner = {"col": 1 - core}
    here, peers = [], []
    for stride in (1, ring, ring * ring):
        q = lax.rem(lax.div(row, stride), ring)
        here.append(q)
        group = []
        for k in range(1, ring):
            there = lax.rem(q + k, ring)
            group.append((k - 1, there, {"row": row + (there - q) * stride}))
        peers.append(group)

    def remote(src, dst, send, recv, device):
        return pltpu.make_async_remote_copy(
            src_ref=src, dst_ref=dst, send_sem=send, recv_sem=recv, device_id=device, device_id_type=MESH
        )

    def half_of(s):
        return core if s else 1 - core

    bases = (0, 0, tokens // 2)
    shares = (tq, aq, aq)
    halves = (th, ah, ah)

    def token_start(axis, q, h):
        return pl.multiple_of(bases[axis] + q * shares[axis] + h * halves[axis], 128)

    def norm_load(src, dst, sem, s, i):
        start = pl.multiple_of(here[0] * tq + half_of(s) * th + i * ct, 128)
        return pltpu.make_async_copy(src.at[pl.ds(start, ct), :], dst.at[s, pl.ds(i * ct, ct), :], sem.at[s, i])

    def down_load(axis, dst, sem, s):
        start = token_start(axis, here[axis], half_of(s))
        return pltpu.make_async_copy(dyd.at[pl.ds(start, ah), :], dst.at[s], sem.at[s])

    x_src = (xn, xa, xa)
    x_dst = (xrn, xra, xrb)

    def x_piece(axis, q, h):
        return x_src[axis].at[:, pl.ds(token_start(axis, q, h), halves[axis])]

    for s in (0, 1):
        for i in range(n_ct):
            norm_load(dyg, dyg_v, ldg, s, i).start()
            norm_load(dyu, dyu_v, ldu, s, i).start()
        down_load(1, dya_v, lda, s).start()
        down_load(2, dyb_v, ldb, s).start()
    own_x = [
        pltpu.make_async_copy(x_piece(a, here[a], h), x_dst[a].at[h, here[a]], ldx.at[a, h])
        for a in range(3)
        for h in (0, 1)
    ]
    for copy in own_x:
        copy.start()

    wn_v[here[0]] = jnp.concatenate([w_gate[...], w_up[...]], axis=0).astype(BF16)
    wa_v[here[1]] = w_down[...].astype(BF16)
    wb_v[here[2]] = w_down[...].astype(BF16)

    barrier = pltpu.get_barrier_semaphore()
    pl.semaphore_signal(barrier, inc=1, device_id=partner, device_id_type=MESH)
    for group in peers:
        for _, _, device in group:
            pl.semaphore_signal(barrier, inc=1, device_id=device, device_id_type=MESH)
    pl.semaphore_wait(barrier, 1 + 3 * (ring - 1))

    w_bufs = (wn_v, wa_v, wb_v)
    w_sends, x_sends = [], []
    for a in range(3):
        for j, there, device in peers[a]:
            slot = w_bufs[a].at[here[a]]
            w_sends.append(remote(slot, slot, w_ss.at[a, j], w_rs.at[a, j], device))
    for j in range(ring - 1):
        for a in range(3):
            _, there, device = peers[a][j]
            x_sends.append(
                remote(x_piece(a, there, core), x_dst[a].at[core, here[a]], x_ss.at[a, j], x_rs.at[a, j], device)
            )
    for copy in w_sends:
        copy.start()
    for copy in x_sends:
        copy.start()

    beta = hyper[0]
    rho = hyper[1]
    bound = hyper[2]
    rc_g, rc_u, rc_d = to_column(r_gate), to_column(r_up), to_column(r_down)
    w_sq = [jnp.sum(w[...] * w[...]).reshape(1, 1) for w in (w_gate, w_up, w_down)]

    for copy in w_sends:
        copy.wait_recv()
    stacked = [wn_v[p].astype(F32) for p in range(ring)]
    wlg_v[...] = jnp.concatenate([v[:m] for v in stacked], axis=0).astype(BF16)
    wlu_v[...] = jnp.concatenate([v[m:] for v in stacked], axis=0).astype(BF16)

    def dx_norm(s, out):
        @pl.loop(0, n_ct)
        def _(i):
            norm_load(dyg, dyg_v, ldg, s, i).wait()
            norm_load(dyu, dyu_v, ldu, s, i).wait()
            part = pl.ds(pl.multiple_of(i * ct, ct), ct)
            out[:, part] = dot_nt(wlg_v[...], dyg_v[s, part, :]) + dot_nt(wlu_v[...], dyu_v[s, part, :])

    def dx_down(axis, s, dy_v, sem, w_v, out):
        down_load(axis, dy_v, sem, s).wait()
        out[...] = dot_nt(w_v[...].reshape(ring * ma, nd), dy_v[s])

    part_sends = [remote(src, dst, p_ss.at[a], p_rs.at[a], partner) for a, (src, dst) in enumerate(((dsn, drn), (dsa, dra), (dsb, drb)))]
    dx_norm(0, dsn)
    part_sends[0].start()
    dx_down(1, 0, dya_v, lda, wa_v, dsa)
    part_sends[1].start()
    dx_down(2, 0, dyb_v, ldb, wb_v, dsb)
    part_sends[2].start()

    dx_out = (dxn_o, dxa_o, dxa_o)
    fins = (fin_n, fin_a, fin_b)

    def out_piece(axis, q, h):
        return dx_out[axis].at[:, pl.ds(token_start(axis, q, h), halves[axis])]

    dx_sends, own_sends, own_copies = [], [], []
    for a in range(3):
        target = out_piece(a, here[a], core)
        own = fins[a].at[here[a]]
        own_sends.append(remote(own, target, o_ss.at[a], o_rs.at[a], partner))
        own_copies.append(pltpu.make_async_copy(own, target, o_ls.at[a]))
        for j, there, device in peers[a]:
            dx_sends.append(remote(fins[a].at[there], target, d_ss.at[a, j], d_rs.at[a, j], device))

    def finish(a, kept, got):
        part_sends[a].wait_recv()
        total = (kept[...] + got[...]).astype(BF16)
        size = fins[a].shape[1]
        for p in range(ring):
            fins[a][p] = total[p * size : (p + 1) * size]
        for copy in dx_sends[a * (ring - 1) : (a + 1) * (ring - 1)]:
            copy.start()
        own_sends[a].start()
        own_copies[a].start()

    dx_norm(1, dkn)
    finish(0, dkn, drn)
    dx_down(1, 1, dya_v, lda, wa_v, dka)
    finish(1, dka, dra)
    dx_down(2, 1, dyb_v, ldb, wb_v, dkb)
    finish(2, dkb, drb)

    x_forwards = []
    for j in range(ring - 1):
        for a in range(3):
            origin = lax.rem(here[a] + ring - (j + 1), ring)
            slot = x_dst[a].at[core, origin]
            x_forwards.append(remote(slot, slot, xf_ss.at[a, j], xf_rs.at[a, j], partner))
    for got, forward in zip(x_sends, x_forwards, strict=True):
        got.wait_recv()
        forward.start()
    for copy in own_x:
        copy.wait()
    for forward in x_forwards:
        forward.wait_recv()

    for h in (0, 1):
        xln[h] = jnp.concatenate([xrn[h, p].astype(F32) for p in range(ring)], axis=0).astype(BF16)
    grads = []
    for dy_v in (dyg_v, dyu_v):
        grads.append(sum(dot_nn(xln[half_of(s)], dy_v[s]) for s in (0, 1)))
    for p in range(ring):
        gpn[p] = jnp.concatenate([g[p * m : (p + 1) * m] for g in grads], axis=0)
    for x_v, dy_v, out in ((xra, dya_v, gpa), (xrb, dyb_v, gpb)):
        total = sum(dot_nn(x_v[half_of(s)].reshape(ring * ma, ah), dy_v[s]) for s in (0, 1))
        out[...] = total.reshape(ring, ma, nd)
    g_sends = []
    for a, (src, dst) in enumerate(((gpn, grn), (gpa, gra), (gpb, grb))):
        for j, there, device in peers[a]:
            g_sends.append(remote(src.at[there], dst.at[here[a]], g_ss.at[a, j], g_rs.at[a, j], device))
    for copy in g_sends:
        copy.start()
    grn[here[0]] = gpn[here[0]]
    gra[here[1]] = gpa[here[1]]
    grb[here[2]] = gpb[here[2]]

    dx_forwards = []
    for a in range(3):
        for j, _, _ in peers[a]:
            origin = lax.rem(here[a] + ring - (j + 1), ring)
            piece = out_piece(a, origin, core)
            dx_forwards.append(remote(piece, piece, f_ss.at[a, j], f_rs.at[a, j], partner))
    for got, forward in zip(dx_sends, dx_forwards, strict=True):
        got.wait_recv()
        forward.start()

    for copy in g_sends:
        copy.wait_recv()
    g_n = sum(grn[p] for p in range(ring))
    g_g, g_u = g_n[:m], g_n[m:]
    g_d = sum(gra[p] for p in range(ring)) + sum(grb[p] for p in range(ring))
    sq = [g * g for g in (g_g, g_u, g_d)]

    offset = 0
    for v in sq:
        size = v.shape[0]
        rs_v[offset : offset + size, :] = jnp.broadcast_to(jnp.sum(v + EPS_ONE, axis=1, keepdims=True), (size, 128))
        offset += size
    row_swap = remote(rs_v, rr_v, r_ss, r_rs, partner)
    row_swap.start()
    row_swap.wait_recv()
    row_sum = rs_v[...] + rr_v[...]
    r_g = beta * rc_g + (1.0 - beta) * (row_sum[:m] / (cores * nf))
    r_u = beta * rc_u + (1.0 - beta) * (row_sum[m : 2 * m] / (cores * nf))
    r_d = beta * rc_d + (1.0 - beta) * (row_sum[2 * m :] / (cores * nd))
    r_gate_o[...] = to_row(r_g)
    r_up_o[...] = to_row(r_u)
    r_down_o[...] = to_row(r_d)

    wide = [widen(r, v.shape[1]) for r, v in zip((r_g, r_u, r_d), sq, strict=True)]
    st_v[...] = jnp.zeros_like(st_v)
    for i in (0, 1):
        st_v[0, 2 * i : 2 * i + 1, :] = jnp.sum(sq[i] + EPS_ONE, axis=0, keepdims=True)
        st_v[0, 2 * i + 1 : 2 * i + 2, :] = jnp.sum(sq[i] / wide[i], axis=0, keepdims=True)
    st_v[0, 4:5, :nd] = jnp.sum(sq[2] + EPS_ONE, axis=0, keepdims=True)
    st_v[0, 4:5, nd:] = jnp.sum(sq[2] / wide[2], axis=0, keepdims=True)
    for i, r in enumerate((r_g, r_u, r_d)):
        st_v[0, 5:6, i * 128 : (i + 1) * 128] = jnp.sum(r, axis=0, keepdims=True)
        st_v[0, 6:7, i * 128 : (i + 1) * 128] = jnp.broadcast_to(w_sq[i], (1, 128))
    stat_sends = []
    for a in range(3):
        sends = [
            remote(st_v.at[a], sr_v.at[a, here[a]], s_ss.at[a, j], s_rs.at[a, j], device) for j, _, device in peers[a]
        ]
        stat_sends += sends
        for copy in sends:
            copy.start()
        sr_v[a, here[a]] = st_v[a]
        for copy in sends:
            copy.wait_recv()
        total = sum(sr_v[a, p] for p in range(ring))
        if a < 2:
            st_v[a + 1] = total

    c_g = beta * c_gate[...] + (1.0 - beta) * (total[0:1] / (rows * m))
    c_u = beta * c_up[...] + (1.0 - beta) * (total[2:3] / (rows * m))
    c_d = beta * c_down[...] + (1.0 - beta) * (total[4:5, :nd] / (rows * ma))
    c_gate_o[...] = c_g
    c_up_o[...] = c_u
    c_down_o[...] = c_d
    r_mean = [total[5:6, i * 128 : (i + 1) * 128] / (rows * size) for i, size in enumerate((m, m, ma))]
    ratio = (total[1:2] / c_g, total[3:4] / c_u, total[4:5, nd:] / c_d)
    for i in range(3):
        fs_v[i : i + 1, :] = jnp.sum(ratio[i], axis=1, keepdims=True) * r_mean[i]
        fs_v[i + 3 : i + 4, :] = total[6:7, i * 128 : (i + 1) * 128]
    fs_v[6:8, :] = jnp.zeros((2, 128), F32)
    last_swap = remote(fs_v, fr_v, e_ss, e_rs, partner)
    last_swap.start()
    scaled = []
    for g, r, c, mean in zip((g_g, g_u, g_d), wide, (c_g, c_u, c_d), r_mean, strict=True):
        scaled.append(g * lax.rsqrt(r * c / widen(mean, g.shape[1])))
    last_swap.wait_recv()
    sums = fs_v[...] + fr_v[...]
    for i, (w, out) in enumerate(((w_gate, w_gate_o), (w_up, w_up_o), (w_down, w_down_o))):
        count = rows * cores * w.shape[0] * w.shape[1]
        rms_u = jnp.sqrt(sums[i : i + 1] / count)
        rms_w = jnp.sqrt(sums[i + 3 : i + 4] / count)
        factor = rho * jnp.maximum(EPS_TWO, rms_w) / jnp.maximum(1.0, rms_u / bound)
        out[...] = w[...] - widen(factor, w.shape[1]) * scaled[i]

    for copy in own_sends:
        copy.wait_recv()
    for copy in dx_forwards:
        copy.wait_recv()
    for copy in own_copies:
        copy.wait()
    for copy in (*w_sends, *x_sends, *x_forwards, *part_sends, *dx_sends, *own_sends, *dx_forwards, *g_sends, *stat_sends):
        copy.wait_send()
    row_swap.wait_send()
    last_swap.wait_send()


def solution(mesh):
    row_size = mesh.shape["row"]
    cores = mesh.shape["col"]
    ring = round(row_size ** (1 / 3))
    weight_spec = P("row", "col")
    act_spec = P(None, "row")
    grad_spec = P(None, "col")
    in_specs = (weight_spec,) * 3 + (act_spec, act_spec) + (grad_spec,) * 3 + (P("row"), P("col")) * 3 + (P(),)
    out_specs = (weight_spec,) * 3 + (P("row"), P("col")) * 3 + (act_spec, act_spec)

    def body(w_gate, w_up, w_down, x_norm, x_act, dy_gate, dy_up, dy_down, r_gate, c_gate, r_up, c_up, r_down, c_down, hyper_params):
        tokens = x_norm.shape[0]
        m, nf = w_gate.shape
        ma, nd = w_down.shape
        th = tokens // ring // 2
        ah = th // 2
        n_ct = th // min(2048, th)
        peers = ring - 1
        dma = pltpu.SemaphoreType.DMA
        vmem = pl.BlockSpec(memory_space=pltpu.VMEM)
        anywhere = pl.BlockSpec(memory_space=pl.ANY)
        f32 = lambda *shape: jax.ShapeDtypeStruct(shape, F32)
        scratch = [
            pltpu.VMEM((2, th, nf), BF16), pltpu.VMEM((2, th, nf), BF16), pltpu.VMEM((2, ah, nd), BF16), pltpu.VMEM((2, ah, nd), BF16),
            pltpu.VMEM((ring, 2 * m, nf), BF16), pltpu.VMEM((ring, ma, nd), BF16), pltpu.VMEM((ring, ma, nd), BF16),
            pltpu.VMEM((ring * m, nf), BF16), pltpu.VMEM((ring * m, nf), BF16),
            pltpu.VMEM((2, ring, m, th), BF16), pltpu.VMEM((2, ring, ma, ah), BF16), pltpu.VMEM((2, ring, ma, ah), BF16),
            pltpu.VMEM((2, ring * m, th), BF16),
            *[pltpu.VMEM(shape, F32) for _ in range(3) for shape in ((ring * m, th), (ring * ma, ah), (ring * ma, ah))],
            pltpu.VMEM((ring, m, th), BF16), pltpu.VMEM((ring, ma, ah), BF16), pltpu.VMEM((ring, ma, ah), BF16),
            *[pltpu.VMEM(shape, F32) for _ in range(2) for shape in ((ring, 2 * m, nf), (ring, ma, nd), (ring, ma, nd))],
            pltpu.VMEM((2 * m + ma, 128), F32), pltpu.VMEM((2 * m + ma, 128), F32),
            pltpu.VMEM((3, 8, nf), F32), pltpu.VMEM((3, ring, 8, nf), F32),
            pltpu.VMEM((8, 128), F32), pltpu.VMEM((8, 128), F32),
            dma((2, n_ct)), dma((2, n_ct)), dma((2,)), dma((2,)), dma((3, 2)),
            *[dma((3, peers))] * 6, dma((3,)), dma((3,)), dma((3, peers)), dma((3, peers)),
            dma((3,)), dma((3,)), dma((3,)), dma((3, peers)), dma((3, peers)),
            dma((3, peers)), dma((3, peers)), dma, dma, dma((3, peers)), dma((3, peers)), dma, dma,
        ]
        outs = pl.pallas_call(
            functools.partial(step_kernel, (ring, cores, tokens)),
            out_shape=(
                f32(m, nf), f32(m, nf), f32(ma, nd), f32(1, m), f32(1, nf), f32(1, m), f32(1, nf), f32(1, ma), f32(1, nd),
                jax.ShapeDtypeStruct((m, tokens), BF16), jax.ShapeDtypeStruct((ma, tokens), BF16),
            ),
            in_specs=[pl.BlockSpec(memory_space=pltpu.SMEM)] + [vmem] * 3 + [anywhere] * 5 + [vmem] * 6,
            out_specs=(vmem,) * 9 + (anywhere,) * 2,
            scratch_shapes=scratch,
            compiler_params=pltpu.CompilerParams(collective_id=0, has_side_effects=True),
            name="adafactor_step",
        )(
            hyper_params, w_gate, w_up, w_down, x_norm.T, x_act.T, dy_gate, dy_up, dy_down,
            r_gate.reshape(1, -1), c_gate.reshape(1, -1), r_up.reshape(1, -1), c_up.reshape(1, -1),
            r_down.reshape(1, -1), c_down.reshape(1, -1),
        )
        new, stats, (dxn, dxa) = outs[:3], outs[3:9], outs[9:]
        return (*new, *(s.reshape(-1) for s in stats), dxn.T, dxa.T)

    return jax.shard_map(body, mesh=mesh, in_specs=in_specs, out_specs=out_specs, check_vma=False)
```

time: 359 us -> 60.6 us (0.17)
  blocking collectives: 259 us -> 0 us
  matrix products: 77.6 us -> 0 us
  Pallas kernels: 0 us -> 44.1 us
  local copies, waits for them, and re-layouts: 0.78 us -> 15.3 us
  between operations: 11.4 us -> 0.66 us
  other arithmetic: 9.8 us -> 0 us
    psum x3 -> x0, blocking collectives: 259 us -> none  [the longest x1 156 us: factored_step(): r_mean = lax.psum(jnp.sum(r_new), 'row') / m_total]
    dot_general x6 -> x0, matrix products: 77.6 us -> none  [the longest x3 41.4 us: input_grad(): lax.dot_general(grad_out, weight.astype(jnp.bfloat16), (((1,), (1,)), (()...]
    pallas_call x0 -> x1, Pallas kernels: none -> 44.1 us  [body(): pl.pallas_call(functools.partial(step_kernel, (ring, cores, tokens)), out...]
    unnamed x38 -> x11, local copies, waits for them, and re-layouts: 0.12 us -> 15.3 us
    reduce_sum x7 -> x0, other arithmetic: 5.77 us -> none  [the longest x2 2.5 us: factored_step(): r_mean = lax.psum(jnp.sum(r_new), 'row') / m_total]
where the time goes in v1:
time: 60.6 us; the launch traced here: 60.1 us
  Pallas kernels  44.1 us (73%)
  local copies, waits for them, and re-layouts  15.3 us (25%)
  between operations  0.66 us (1%)
    pallas_call x1, Pallas kernels, body(): pl.pallas_call(functools.partial(step_kernel, (ring, cores, tokens)), out...  44.1 us
    unnamed x11, local copies, waits for them, and re-layouts  15.3 us

profile of v1, /device:TPU:1, one launch (start us, length us, event | category | flops | bytes accessed | tf_op | source)
XLA Modules:
  0.0 60.1 jit_solution(11187949241539747282)
XLA Ops:
  0.6 44.1 %adafactor_step.1 = (f32[8,512]{1,0:T(8,128)}, f32[8,512]{1,0:T(8,128)}, f32[16,256]{1,0:T(8,128)}, f32[1,8]{1,0:T(1,128)}, f32[1,512]{1,0:T(1,128)}, /*index=5*...) custom-call(f32[3]{0:T(128)} %hyper.1, ...), custom_call_target="tpu_custom_call" | custom-call | tf_op jit(solution)/shard_map/adafactor_step/pallas_call | solution.py:385
  44.7 1.3 %copy.37 = f32[8,512]{1,0:T(8,128)} copy(f32[8,512]{1,0:T(8,128)} %get-tuple-element.44) | data formatting | bytes 32768
  46.1 1.3 %copy.38 = f32[8,512]{1,0:T(8,128)} copy(f32[8,512]{1,0:T(8,128)} %get-tuple-element.45) | data formatting | bytes 32768
  47.4 1.3 %copy.39 = f32[16,256]{1,0:T(8,128)} copy(f32[16,256]{1,0:T(8,128)} %get-tuple-element.46) | data formatting | bytes 32768
  48.7 1.2 %copy.40 = f32[8]{0:T(128)} copy(f32[8]{0:T(128)} %bitcast.31) | data formatting | bytes 64
  49.9 1.3 %copy.41 = f32[512]{0:T(512)} copy(f32[512]{0:T(512)} %bitcast.23) | data formatting | bytes 4096
  51.1 1.1 %copy.42 = f32[8]{0:T(128)} copy(f32[8]{0:T(128)} %bitcast.30) | data formatting | bytes 64
  52.3 1.3 %copy.43 = f32[512]{0:T(512)} copy(f32[512]{0:T(512)} %bitcast.22) | data formatting | bytes 4096
  53.5 1.2 %copy.44 = f32[16]{0:T(128)} copy(f32[16]{0:T(128)} %bitcast.29) | data formatting | bytes 128
  54.7 1.2 %copy.45 = f32[256]{0:T(256)} copy(f32[256]{0:T(256)} %bitcast.24) | data formatting | bytes 2048
  55.9 1.9 %copy.46 = bf16[32768,8]{0,1:T(8,128)(2,1)} copy(bf16[32768,8]{0,1:T(8,128)(2,1)} %bitcast.19) | data formatting | bytes 1048576
  57.8 2.3 %copy.47 = bf16[32768,16]{0,1:T(8,128)(2,1)} copy(bf16[32768,16]{0,1:T(8,128)(2,1)} %bitcast.17) | data formatting | bytes 2097152

commit v2 on v1

v2 whole, which is shorter than its diff:
```python
import functools

import jax
import jax.numpy as jnp
from jax import lax
from jax.experimental import pallas as pl
from jax.experimental.pallas import tpu as pltpu
from jax.sharding import PartitionSpec as P

EPS_ONE = 1e-30
EPS_TWO = 1e-3
MESH = pl.DeviceIdType.MESH
BF16 = jnp.bfloat16
F32 = jnp.float32


def dot_nt(lhs, rhs):
    return lax.dot_general(lhs, rhs, (((1,), (1,)), ((), ())), preferred_element_type=F32)


def dot_nn(lhs, rhs):
    return lax.dot_general(lhs, rhs, (((1,), (0,)), ((), ())), preferred_element_type=F32)


def to_column(row_ref):
    m = row_ref.shape[1]
    eye = lax.broadcasted_iota(jnp.int32, (m, m), 0) == lax.broadcasted_iota(jnp.int32, (m, m), 1)
    spread = jnp.where(eye, jnp.broadcast_to(row_ref[...], (m, m)), 0.0)
    return jnp.broadcast_to(jnp.sum(spread, axis=1, keepdims=True), (m, 128))


def to_row(column):
    m = column.shape[0]
    eye = lax.broadcasted_iota(jnp.int32, (m, m), 0) == lax.broadcasted_iota(jnp.int32, (m, m), 1)
    return jnp.sum(jnp.where(eye, column[:, :m], 0.0), axis=0, keepdims=True)


def widen(column, n):
    return jnp.concatenate([column] * (n // 128), axis=1)


def step_kernel(
    dims,
    hyper_in, w_gate, w_up, w_down, xn, xa, dyg, dyu, dyd, r_gate, c_gate, r_up, c_up, r_down, c_down,
    w_gate_o, w_up_o, w_down_o, r_gate_o, c_gate_o, r_up_o, c_up_o, r_down_o, c_down_o, dxn_o, dxa_o,
    dyg_v, dyu_v, dya_v, dyb_v,
    wg_v, wu_v, wd_v, rg_v, cg_v, ru_v, cu_v, rd_v, cd_v, hyper,
    wn_v, wa_v, wb_v, wlg_v, wlu_v,
    xrn, xra, xrb, xln,
    dsn, dsa, dsb, dkn, dka, dkb, drn, dra, drb, fin_n, fin_a, fin_b,
    gpn, gpa, gpb, grn, gra, grb,
    st_v, sr_v, cc_v, res_v,
    ldg, ldu, lda, ldb, ldx, lds,
    w_ss, w_rs, x_ss, x_rs, xf_ss, xf_rs, p_ss, p_rs, d_ss, d_rs, o_ss, o_rs, f_ss, f_rs,
    g_ss, g_rs, y_ss, y_rs, s_ss, s_rs, c_ss, c_rs, e_ss, e_rs,
):
    ring, cores, tokens = dims
    m, nf = w_gate.shape
    ma, nd = w_down.shape
    tq = tokens // ring
    th = tq // 2
    aq = tq // 2
    ah = aq // 2
    ct = min(2048, th)
    n_ct = th // ct
    rows = ring**3
    chief = cores - 1

    core = lax.axis_index("col")
    row = lax.axis_index("row")
    partner = {"col": 1 - core}
    here, peers = [], []
    for stride in (1, ring, ring * ring):
        q = lax.rem(lax.div(row, stride), ring)
        here.append(q)
        group = []
        for k in range(1, ring):
            there = lax.rem(q + k, ring)
            group.append((k - 1, there, row + (there - q) * stride))
        peers.append(group)

    def remote(src, dst, send, recv, device):
        return pltpu.make_async_remote_copy(
            src_ref=src, dst_ref=dst, send_sem=send, recv_sem=recv, device_id=device, device_id_type=MESH
        )

    def half_of(s):
        return core if s else 1 - core

    bases = (0, 0, tokens // 2)
    shares = (tq, aq, aq)
    halves = (th, ah, ah)

    def token_start(axis, q, h):
        return pl.multiple_of(bases[axis] + q * shares[axis] + h * halves[axis], 128)

    def norm_load(src, dst, sem, s, i):
        start = pl.multiple_of(here[0] * tq + half_of(s) * th + i * ct, 128)
        return pltpu.make_async_copy(src.at[pl.ds(start, ct), :], dst.at[s, pl.ds(i * ct, ct), :], sem.at[s, i])

    def down_load(axis, dst, sem, s):
        start = token_start(axis, here[axis], half_of(s))
        return pltpu.make_async_copy(dyd.at[pl.ds(start, ah), :], dst.at[s], sem.at[s])

    x_src = (xn, xa, xa)
    x_dst = (xrn, xra, xrb)

    def x_piece(axis, q, h):
        return x_src[axis].at[:, pl.ds(token_start(axis, q, h), halves[axis])]

    barrier = pltpu.get_barrier_semaphore()
    pl.semaphore_signal(barrier, inc=1, device_id=partner, device_id_type=MESH)
    for group in peers:
        for _, _, device in group:
            pl.semaphore_signal(barrier, inc=1, device_id={"row": device}, device_id_type=MESH)

    small = [
        pltpu.make_async_copy(src, dst, lds.at[i])
        for i, (src, dst) in enumerate(
            ((w_gate, wg_v), (w_up, wu_v), (w_down, wd_v), (r_gate, rg_v), (c_gate, cg_v), (r_up, ru_v), (c_up, cu_v), (r_down, rd_v), (c_down, cd_v), (hyper_in, hyper))
        )
    ]
    for copy in small:
        copy.start()
    for copy in small:
        copy.wait()
    loads = []
    for s in (0, 1):
        group = []
        for i in range(n_ct):
            group += [norm_load(dyg, dyg_v, ldg, s, i), norm_load(dyu, dyu_v, ldu, s, i)]
        group += [down_load(1, dya_v, lda, s), down_load(2, dyb_v, ldb, s)]
        for copy in group:
            copy.start()
        loads.append(group)
    own_x = [
        pltpu.make_async_copy(x_piece(a, here[a], h), x_dst[a].at[h, here[a]], ldx.at[a, h])
        for a in range(3)
        for h in (0, 1)
    ]
    for copy in own_x:
        copy.start()

    wn_v[here[0]] = jnp.concatenate([wg_v[...], wu_v[...]], axis=0).astype(BF16)
    wa_v[here[1]] = wd_v[...].astype(BF16)
    wb_v[here[2]] = wd_v[...].astype(BF16)
    cc_v[0] = jnp.zeros(cc_v.shape[1:], F32)
    cc_v[0, 0:1, :] = cg_v[...]
    cc_v[0, 1:2, :] = cu_v[...]
    cc_v[0, 2:3, :nd] = cd_v[...]
    for i, w in enumerate((wg_v, wu_v, wd_v)):
        cc_v[0, 3:4, i * 128 : (i + 1) * 128] = jnp.broadcast_to(jnp.sum(w[...] * w[...]).reshape(1, 1), (1, 128))

    pl.semaphore_wait(barrier, 1 + 3 * (ring - 1))

    w_bufs = (wn_v, wa_v, wb_v)
    w_sends, x_sends = [], []
    for a in range(3):
        for j, there, device in peers[a]:
            slot = w_bufs[a].at[here[a]]
            w_sends.append(remote(slot, slot, w_ss.at[a, j], w_rs.at[a, j], {"row": device}))
    for j in range(ring - 1):
        for a in range(3):
            _, there, device = peers[a][j]
            x_sends.append(
                remote(x_piece(a, there, core), x_dst[a].at[core, here[a]], x_ss.at[a, j], x_rs.at[a, j], {"row": device})
            )
    for copy in w_sends:
        copy.start()
    for copy in x_sends:
        copy.start()

    for copy in w_sends:
        copy.wait_recv()
    stacked = [wn_v[p].astype(F32) for p in range(ring)]
    wlg_v[...] = jnp.concatenate([v[:m] for v in stacked], axis=0).astype(BF16)
    wlu_v[...] = jnp.concatenate([v[m:] for v in stacked], axis=0).astype(BF16)

    cc_send = remote(cc_v.at[0], cc_v.at[1], c_ss, c_rs, partner)

    @pl.when(core != chief)
    def _():
        cc_send.start()

    def dx_norm(s, out):
        for i in range(n_ct):
            part = slice(i * ct, (i + 1) * ct)
            out[:, part] = dot_nt(wlg_v[...], dyg_v[s, part, :]) + dot_nt(wlu_v[...], dyu_v[s, part, :])

    def dx_down(s, dy_v, w_v, out):
        out[...] = dot_nt(w_v[...].reshape(ring * ma, nd), dy_v[s])

    part_sends = [
        remote(src, dst, p_ss.at[a], p_rs.at[a], partner) for a, (src, dst) in enumerate(((dsn, drn), (dsa, dra), (dsb, drb)))
    ]
    for copy in loads[0]:
        copy.wait()
    dx_norm(0, dsn)
    dx_down(0, dya_v, wa_v, dsa)
    dx_down(0, dyb_v, wb_v, dsb)
    for copy in part_sends:
        copy.start()
    for copy in loads[1]:
        copy.wait()

    dx_out = (dxn_o, dxa_o, dxa_o)
    fins = (fin_n, fin_a, fin_b)

    def out_piece(axis, q, h):
        return dx_out[axis].at[:, pl.ds(token_start(axis, q, h), halves[axis])]

    dx_sends, own_sends = [], []
    for a in range(3):
        target = out_piece(a, here[a], core)
        own_sends.append(remote(target, target, o_ss.at[a], o_rs.at[a], partner))
        for j, there, device in peers[a]:
            dx_sends.append(remote(fins[a].at[there], target, d_ss.at[a, j], d_rs.at[a, j], {"row": device}))

    def finish(a, kept, got):
        part_sends[a].wait_recv()
        total = (kept[...] + got[...]).astype(BF16)
        size = fins[a].shape[1]
        for p in range(ring):
            fins[a][p] = total[p * size : (p + 1) * size]
        dx_out[a][:, pl.ds(token_start(a, here[a], core), halves[a])] = fins[a][here[a]]
        for copy in dx_sends[a * (ring - 1) : (a + 1) * (ring - 1)]:
            copy.start()
        own_sends[a].start()

    dx_norm(1, dkn)
    finish(0, dkn, drn)

    x_forwards = []
    for j in range(ring - 1):
        for a in range(3):
            origin = lax.rem(here[a] + ring - (j + 1), ring)
            slot = x_dst[a].at[core, origin]
            x_forwards.append(remote(slot, slot, xf_ss.at[a, j], xf_rs.at[a, j], partner))
    for got, forward in zip(x_sends, x_forwards, strict=True):
        got.wait_recv()
        forward.start()
    for copy in own_x:
        copy.wait()

    def grads_of(s):
        h = half_of(s)
        xln[s] = jnp.concatenate([xrn[h, p].astype(F32) for p in range(ring)], axis=0).astype(BF16)
        return (
            dot_nn(xln[s], dyg_v[s]),
            dot_nn(xln[s], dyu_v[s]),
            dot_nn(xra[h].reshape(ring * ma, ah), dya_v[s]),
            dot_nn(xrb[h].reshape(ring * ma, ah), dyb_v[s]),
        )

    def put_grads(values, add):
        g_g, g_u, g_a, g_b = values
        for p in range(ring):
            for i, g in enumerate((g_g, g_u)):
                piece = g[p * m : (p + 1) * m]
                gpn[p, i * m : (i + 1) * m, :] = gpn[p, i * m : (i + 1) * m, :] + piece if add else piece
        for out, g in ((gpa, g_a), (gpb, g_b)):
            g = g.reshape(ring, ma, nd)
            out[...] = out[...] + g if add else g

    put_grads(grads_of(1), False)

    for forward in x_forwards:
        forward.wait_recv()

    put_grads(grads_of(0), True)

    g_bufs = ((gpn, grn), (gpa, gra), (gpb, grb))
    g_sends = [
        remote(src.at[there], dst.at[core, here[a]], g_ss.at[a, j], g_rs.at[core, a, j], {"row": device, "col": chief})
        for a, (src, dst) in enumerate(g_bufs)
        for j, there, device in peers[a]
    ]
    y_sends = [
        remote(src.at[here[a]], dst.at[core, here[a]], y_ss.at[a], y_rs.at[a], partner) for a, (src, dst) in enumerate(g_bufs)
    ]
    for copy in g_sends:
        copy.start()

    @pl.when(core != chief)
    def _():
        for copy in y_sends:
            copy.start()

    @pl.when(core == chief)
    def _():
        for a, (src, dst) in enumerate(g_bufs):
            dst[chief, here[a]] = src[here[a]]

    dx_down(1, dya_v, wa_v, dka)
    dx_down(1, dyb_v, wb_v, dkb)
    finish(1, dka, dra)
    finish(2, dkb, drb)

    dx_forwards = []
    for a in range(3):
        for j, _, _ in peers[a]:
            origin = lax.rem(here[a] + ring - (j + 1), ring)
            piece = out_piece(a, origin, core)
            dx_forwards.append(remote(piece, piece, f_ss.at[a, j], f_rs.at[a, j], partner))

    def forward_dx(axes):
        for a in axes:
            for j in range(ring - 1):
                dx_sends[a * (ring - 1) + j].wait_recv()
                dx_forwards[a * (ring - 1) + j].start()

    res_send = remote(res_v, res_v, e_ss, e_rs, partner)
    stat_sends = [
        [remote(st_v.at[a], sr_v.at[a, here[a]], s_ss.at[a, j], s_rs.at[a, j], {"row": device}) for j, _, device in peers[a]]
        for a in range(3)
    ]
    down_row = 2 * m
    last_row = 2 * m + ma

    @pl.when(core != chief)
    def _():
        forward_dx((0, 1, 2))
        res_send.wait_recv()
        w_gate_o[...] = wg_v[...] - res_v[0:m, :]
        w_up_o[...] = wu_v[...] - res_v[m : 2 * m, :]
        w_down_o[...] = wd_v[...] - res_v[down_row:last_row, :nd]
        c_gate_o[...] = res_v[last_row : last_row + 1, :]
        c_up_o[...] = res_v[last_row + 1 : last_row + 2, :]
        c_down_o[...] = res_v[last_row + 2 : last_row + 3, :nd]
        r_gate_o[...] = res_v[last_row + 3 : last_row + 4, 0:m]
        r_up_o[...] = res_v[last_row + 3 : last_row + 4, 128 : 128 + m]
        r_down_o[...] = res_v[last_row + 3 : last_row + 4, 256 : 256 + ma]
        for copies in (y_sends, [cc_send]):
            for copy in copies:
                copy.wait_send()

    @pl.when(core == chief)
    def _():
        beta = hyper[0]
        rho = hyper[1]
        bound = hyper[2]
        rc_g, rc_u, rc_d = to_column(rg_v), to_column(ru_v), to_column(rd_v)
        res_v[last_row:, :] = jnp.zeros((8, nf), F32)
        cc_send.wait_recv()
        for c in range(cores):
            for a, (src, dst) in enumerate(g_bufs):
                for j in range(ring - 1):
                    remote(src.at[0], dst.at[c, 0], g_ss.at[a, j], g_rs.at[c, a, j], partner).wait_recv()
        for copy in y_sends:
            copy.wait_recv()
        grad = []
        for c in range(cores):
            g_n = sum(grn[c, p] for p in range(ring))
            grad.append((g_n[:m], g_n[m:], sum(gra[c, p] for p in range(ring)) + sum(grb[c, p] for p in range(ring))))
        sq = [[g * g for g in gs] for gs in grad]
        sizes = (m, m, ma)
        lanes = (nf, nf, nd)
        r_new, wide = [], []
        for i, r_old in enumerate((rc_g, rc_u, rc_d)):
            row_sum = sum(jnp.sum(sq[c][i] + EPS_ONE, axis=1, keepdims=True) for c in range(cores))
            row_mean = jnp.broadcast_to(row_sum, (sizes[i], 128)) / (cores * lanes[i])
            r_new.append(beta * r_old + (1.0 - beta) * row_mean)
            wide.append(widen(r_new[i], lanes[i]))

        st_v[0] = jnp.zeros(st_v.shape[1:], F32)
        for i in range(3):
            inverse = 1.0 / wide[i]
            for c in range(cores):
                q_sum = jnp.sum(sq[c][i] + EPS_ONE, axis=0, keepdims=True)
                u_sum = jnp.sum(sq[c][i] * inverse, axis=0, keepdims=True)
                if i < 2:
                    st_v[0, 8 * c + 2 * i : 8 * c + 2 * i + 1, :] = q_sum
                    st_v[0, 8 * c + 2 * i + 1 : 8 * c + 2 * i + 2, :] = u_sum
                else:
                    st_v[0, 8 * c + 4 : 8 * c + 5, :nd] = q_sum
                    st_v[0, 8 * c + 4 : 8 * c + 5, nd:] = u_sum
            st_v[0, 5:6, i * 128 : (i + 1) * 128] = jnp.sum(r_new[i], axis=0, keepdims=True)
        st_v[0, 6:7, :] = cc_v[0, 3:4, :] + cc_v[1, 3:4, :]
        total = None
        for a in range(3):
            for copy in stat_sends[a]:
                copy.start()
            sr_v[a, here[a]] = st_v[a]
            if a == 0:
                for i, (r, out) in enumerate(zip(r_new, (r_gate_o, r_up_o, r_down_o), strict=True)):
                    line = to_row(r)
                    out[...] = line
                    res_v[last_row + 3 : last_row + 4, i * 128 : i * 128 + sizes[i]] = line
            forward_dx(((0,), (1, 2), ())[a])
            for copy in stat_sends[a]:
                copy.wait_recv()
            total = sum(sr_v[a, p] for p in range(ring))
            if a < 2:
                st_v[a + 1] = total

        r_mean = [total[5:6, i * 128 : (i + 1) * 128] / (rows * sizes[i]) for i in range(3)]
        factor = []
        c_new = [[], []]
        for i in range(3):
            u_sq = 0.0
            for c in range(cores):
                base = 8 * c
                if i < 2:
                    q_sum = total[base + 2 * i : base + 2 * i + 1]
                    u_sum = total[base + 2 * i + 1 : base + 2 * i + 2]
                else:
                    q_sum = total[base + 4 : base + 5, :nd]
                    u_sum = total[base + 4 : base + 5, nd:]
                c_old = cc_v[0 if c == chief else 1, i : i + 1, : lanes[i]]
                c_new[c].append(beta * c_old + (1.0 - beta) * (q_sum / (rows * sizes[i])))
                u_sq += jnp.sum(u_sum / c_new[c][i], axis=1, keepdims=True)
            count = rows * cores * sizes[i] * lanes[i]
            rms_u = jnp.sqrt(u_sq * r_mean[i] / count)
            rms_w = jnp.sqrt(total[6:7, i * 128 : (i + 1) * 128] / count)
            factor.append(rho * jnp.maximum(EPS_TWO, rms_w) / jnp.maximum(1.0, rms_u / bound))
        for c in range(cores):
            step = []
            for i in range(3):
                v = wide[i] * c_new[c][i] / widen(r_mean[i], lanes[i])
                step.append(widen(factor[i], lanes[i]) * (grad[c][i] * lax.rsqrt(v)))
            if c != chief:
                res_v[0:m, :] = step[0]
                res_v[m : 2 * m, :] = step[1]
                res_v[down_row:last_row, :nd] = step[2]
                res_v[last_row : last_row + 1, :] = c_new[c][0]
                res_v[last_row + 1 : last_row + 2, :] = c_new[c][1]
                res_v[last_row + 2 : last_row + 3, :nd] = c_new[c][2]
                res_send.start()
            else:
                for i, (w, out) in enumerate(((wg_v, w_gate_o), (wu_v, w_up_o), (wd_v, w_down_o))):
                    out[...] = w[...] - step[i]
                for i, out in enumerate((c_gate_o, c_up_o, c_down_o)):
                    out[...] = c_new[c][i]
        for sends in (*stat_sends, [res_send]):
            for copy in sends:
                copy.wait_send()

    for copy in own_sends:
        copy.wait_recv()
    for copy in dx_forwards:
        copy.wait_recv()
    for copy in (*w_sends, *x_sends, *x_forwards, *part_sends, *dx_sends, *own_sends, *dx_forwards, *g_sends):
        copy.wait_send()


def write_kernel(*refs):
    count = (len(refs) - 1) // 2
    sems = refs[-1]
    copies = [pltpu.make_async_copy(refs[i], refs[count + i], sems.at[i]) for i in range(count)]
    for copy in reversed(copies):
        copy.start()
    for copy in copies:
        copy.wait()


def solution(mesh):
    row_size = mesh.shape["row"]
    cores = mesh.shape["col"]
    ring = round(row_size ** (1 / 3))
    weight_spec = P("row", "col")
    act_spec = P(None, "row")
    grad_spec = P(None, "col")
    in_specs = (weight_spec,) * 3 + (act_spec, act_spec) + (grad_spec,) * 3 + (P("row"), P("col")) * 3 + (P(),)
    out_specs = (weight_spec,) * 3 + (P("row"), P("col")) * 3 + (act_spec, act_spec)

    def body(w_gate, w_up, w_down, x_norm, x_act, dy_gate, dy_up, dy_down, r_gate, c_gate, r_up, c_up, r_down, c_down, hyper_params):
        tokens = x_norm.shape[0]
        m, nf = w_gate.shape
        ma, nd = w_down.shape
        th = tokens // ring // 2
        ah = th // 2
        n_ct = th // min(2048, th)
        peers = ring - 1
        dma = pltpu.SemaphoreType.DMA
        vmem = pl.BlockSpec(memory_space=pltpu.VMEM)
        anywhere = pl.BlockSpec(memory_space=pltpu.HBM)
        scratch = [
            pltpu.VMEM((2, th, nf), BF16), pltpu.VMEM((2, th, nf), BF16), pltpu.VMEM((2, ah, nd), BF16), pltpu.VMEM((2, ah, nd), BF16),
            *[pltpu.VMEM(s, F32) for s in ((m, nf), (m, nf), (ma, nd), (1, m), (1, nf), (1, m), (1, nf), (1, ma), (1, nd))],
            pltpu.SMEM((3,), F32),
            pltpu.VMEM((ring, 2 * m, nf), BF16), pltpu.VMEM((ring, ma, nd), BF16), pltpu.VMEM((ring, ma, nd), BF16),
            pltpu.VMEM((ring * m, nf), BF16), pltpu.VMEM((ring * m, nf), BF16),
            pltpu.VMEM((2, ring, m, th), BF16), pltpu.VMEM((2, ring, ma, ah), BF16), pltpu.VMEM((2, ring, ma, ah), BF16),
            pltpu.VMEM((2, ring * m, th), BF16),
            *[pltpu.VMEM(shape, F32) for _ in range(3) for shape in ((ring * m, th), (ring * ma, ah), (ring * ma, ah))],
            pltpu.VMEM((ring, m, th), BF16), pltpu.VMEM((ring, ma, ah), BF16), pltpu.VMEM((ring, ma, ah), BF16),
            *[pltpu.VMEM(s, F32) for s in ((ring, 2 * m, nf), (ring, ma, nd), (ring, ma, nd))],
            *[pltpu.VMEM((cores, *s), F32) for s in ((ring, 2 * m, nf), (ring, ma, nd), (ring, ma, nd))],
            pltpu.VMEM((3, 8 * cores, nf), F32), pltpu.VMEM((3, ring, 8 * cores, nf), F32),
            pltpu.VMEM((2, 8, nf), F32), pltpu.VMEM((2 * m + ma + 8, nf), F32),
            dma((2, n_ct)), dma((2, n_ct)), dma((2,)), dma((2,)), dma((3, 2)), dma((10,)),
            *[dma((3, peers))] * 6, dma((3,)), dma((3,)), dma((3, peers)), dma((3, peers)),
            dma((3,)), dma((3,)), dma((3, peers)), dma((3, peers)),
            dma((3, peers)), dma((cores, 3, peers)), dma((3,)), dma((3,)), dma((3, peers)), dma((3, peers)), dma, dma, dma, dma,
        ]
        shapes = [(s, F32) for s in ((m, nf), (m, nf), (ma, nd), (1, m), (1, nf), (1, m), (1, nf), (1, ma), (1, nd))]
        shapes += [((m, tokens), BF16), ((ma, tokens), BF16)]
        operands = (
            hyper_params, w_gate, w_up, w_down, x_norm.T, x_act.T, dy_gate, dy_up, dy_down,
            r_gate.reshape(1, -1), c_gate.reshape(1, -1), r_up.reshape(1, -1), c_up.reshape(1, -1),
            r_down.reshape(1, -1), c_down.reshape(1, -1),
        )
        held = pl.pallas_call(
            functools.partial(step_kernel, (ring, cores, tokens)),
            out_shape=tuple(pltpu.VMEM(s, d) for s, d in shapes),
            in_specs=[anywhere] * 15,
            out_specs=(vmem,) * len(shapes),
            scratch_shapes=scratch,
            compiler_params=pltpu.CompilerParams(collective_id=0, has_side_effects=True, vmem_limit_bytes=48 * 2**20),
            name="adafactor_step",
        )(*[pltpu.with_memory_space_constraint(v, pltpu.HBM) for v in operands])
        outs = pl.pallas_call(
            write_kernel,
            out_shape=tuple(jax.ShapeDtypeStruct(s, d) for s, d in shapes),
            in_specs=[vmem] * len(shapes),
            out_specs=(anywhere,) * len(shapes),
            scratch_shapes=[dma((len(shapes),))],
            compiler_params=pltpu.CompilerParams(vmem_limit_bytes=4 * 2**20),
            name="write_results",
        )(*held)
        new, stats, (dxn, dxa) = outs[:3], outs[3:9], outs[9:]
        return (*new, *(s.reshape(-1) for s in stats), dxn.T, dxa.T)

    return jax.shard_map(body, mesh=mesh, in_specs=in_specs, out_specs=out_specs, check_vma=False)
```

time: 60.6 us -> 40 us (0.66)
  local copies, waits for them, and re-layouts: 15.3 us -> 0 us
  Pallas kernels: 44.1 us -> 39.1 us
    unnamed x11 -> x0, local copies, waits for them, and re-layouts: 15.3 us -> none
    pallas_call x1, Pallas kernels: 44.1 us -> 37.9 us  [body(): pl.pallas_call(functools.partial(step_kernel, (ring, cores, tokens)), out...]
    pallas_call x0 -> x1, Pallas kernels: none -> 1.28 us  [body(): pl.pallas_call(write_kernel, out_shape=tuple((jax.ShapeDtypeStruct(s, d)...]
where the time goes in v2:
time: 40 us; the launch traced here: 39.8 us
  Pallas kernels  39.1 us (98%)
  between operations  0.66 us (2%)
    pallas_call x1, Pallas kernels, body(): pl.pallas_call(functools.partial(step_kernel, (ring, cores, tokens)), out...  37.9 us
    pallas_call x1, Pallas kernels, body(): pl.pallas_call(write_kernel, out_shape=tuple((jax.ShapeDtypeStruct(s, d)...  1.28 us

profile of v2, /device:TPU:1, one launch (start us, length us, event | category | flops | bytes accessed | tf_op | source)
XLA Modules:
  0.0 39.8 jit_solution(7783878390642421934)
XLA Ops:
  0.6 37.9 %adafactor_step.1 = (f32[8,512]{1,0:T(8,128)S(1)}, f32[8,512]{1,0:T(8,128)S(1)}, f32[16,256]{1,0:T(8,128)S(1)}, f32[1,8]{1,0:T(1,128)S(1)}, f32[1,512]{1,0:T(1,1...) custom-call(f32[3]{0:T(128)} %hyper_in.1, ...), custom_call_target="tpu_custom_call" | custom-call | tf_op jit(solution)/shard_map/adafactor_step/pallas_call | solution.py:503
  38.5 1.3 %write_results.1 = (f32[8,512]{1,0:T(8,128)}, f32[8,512]{1,0:T(8,128)}, f32[16,256]{1,0:T(8,128)}, f32[1,8]{1,0:T(1,128)}, f32[1,512]{1,0:T(1,128)}, /*index=5*/...) custom-call(f32[8,512]{1,0:T(8,128)S(1)} %get-tuple-element.33.refs_, ...), custom_call_target="tpu_custom_call" | custom-call | tf_op jit(solution)/shard_map/write_results/pallas_call | solution.py:512
